TPU v7x, 32 devices: a whole 2x2x4 slice. The times are simulated.
32 devices in a mesh: node: 8 (over y, x, core), grp: 4 (over z).
Axes of the slice: x: 2, y: 2, z: 4, core: 2. Of those that a mesh axis runs over, the one named last changes fastest.
Arguments:
- tokens: bfloat16 [12288, 1792], P(('node', 'grp')), may hold values from -6 to 6
- cotangent: bfloat16 [12288, 1792], P(('node', 'grp')), may hold values from -6 to 6
- gate_weight: bfloat16 [1792, 1024], P('node'), may hold values from -0.125 to 0.125
- up_weight: bfloat16 [1792, 1024], P('node'), may hold values from -0.125 to 0.125
- down_weight_t: bfloat16 [1792, 1024], P('node'), may hold values from -0.125 to 0.125
- error_memory: bfloat16 [4, 1792, 3072], P('grp', 'node'), may hold values from -4 to 4
- q_init: float32 [3, 1024, 32], replicated, may hold values from -6 to 6
Outputs:
- token_grad: bfloat16 [12288, 1792], P(('node', 'grp'))
- new_error: bfloat16 [4, 1792, 3072], P('grp', 'node')
- p_hat: float32 [3, 1792, 32], P(None, 'node')
- q_new: float32 [3, 1024, 32], replicated
All inputs are finite; a program needn't handle non-finite values.
Results may differ from a plain program's by a relative error of at most 0.012.
Values may be sent and summed in bfloat16 or wider, within the bound.
A program may use at most 192 MiB of HBM per device.

v0:
```python
import math
import jax
import jax.numpy as jnp
from jax import lax
from jax.sharding import PartitionSpec as P


def gelu_parts(value):
    coeff = math.sqrt(2.0 / math.pi)
    inner = coeff * (value + 0.044715 * value * value * value)
    tanh_value = jnp.tanh(inner)
    activation = 0.5 * value * (1.0 + tanh_value)
    slope = 0.5 * (1.0 + tanh_value) + 0.5 * value * (1.0 - tanh_value * tanh_value) * coeff * (
        1.0 + 3.0 * 0.044715 * value * value
    )
    return (activation, slope)


def contract_rows(left_side, right_side):
    return lax.dot_general(
        left_side, right_side, (((0,), (0,)), ((), ())), preferred_element_type=jnp.float32
    )


def on_device(tokens, cotangent, gate_weight, up_weight, down_weight_t, error_memory, q_init):
    node_count = lax.axis_size("node")
    group_count = lax.axis_size("grp")
    hidden_units = gate_weight.shape[1]
    highest = lax.Precision.HIGHEST
    full_gate, full_up, full_down = (
        lax.all_gather(gate_weight, "node", axis=0, tiled=True),
        lax.all_gather(up_weight, "node", axis=0, tiled=True),
        lax.all_gather(down_weight_t, "node", axis=0, tiled=True),
    )
    gate_pre = jnp.dot(tokens, full_gate, preferred_element_type=jnp.float32)
    up_pre = jnp.dot(tokens, full_up, preferred_element_type=jnp.float32)
    activation, slope = gelu_parts(gate_pre)
    hidden = (activation * up_pre).astype(jnp.bfloat16)
    back_hidden = jnp.dot(cotangent, full_down, preferred_element_type=jnp.float32)
    grad_up = (back_hidden * activation).astype(jnp.bfloat16)
    grad_gate = (back_hidden * up_pre * slope).astype(jnp.bfloat16)
    token_grad = (
        lax.dot_general(
            grad_gate, full_gate, (((1,), (1,)), ((), ())), preferred_element_type=jnp.float32
        )
        + lax.dot_general(
            grad_up, full_up, (((1,), (1,)), ((), ())), preferred_element_type=jnp.float32
        )
    ).astype(jnp.bfloat16)
    gate_up = jnp.concatenate([grad_gate, grad_up], axis=1)
    token_cols, cot_cols = (
        lax.all_to_all(tokens, "node", split_axis=1, concat_axis=0, tiled=True),
        lax.all_to_all(cotangent, "node", split_axis=1, concat_axis=0, tiled=True),
    )
    piece_gu = lax.all_gather(gate_up, "node", axis=0, tiled=True)
    piece_hidden = lax.all_gather(hidden, "node", axis=0, tiled=True)
    summed = jnp.concatenate(
        [contract_rows(token_cols, piece_gu), contract_rows(cot_cols, piece_hidden)], axis=1
    )
    grad_scale = 1.0 / math.sqrt(tokens.shape[0] * node_count)
    merged = summed * grad_scale + error_memory[0].astype(jnp.float32)
    blocks = [merged[:, m * hidden_units : (m + 1) * hidden_units] for m in range(3)]
    row_terms = jnp.stack([jnp.dot(blocks[m], q_init[m], precision=highest) for m in range(3)])
    power_rows = lax.psum(row_terms.astype(jnp.bfloat16), "grp").astype(jnp.float32) / group_count
    local_gram = jnp.einsum("mdr,mds->mrs", power_rows, power_rows, precision=highest)
    gram_matrix = lax.psum(local_gram, "node")
    hats = []
    for m in range(3):
        factor = jnp.linalg.cholesky(gram_matrix[m])
        hats.append(jax.scipy.linalg.solve_triangular(factor, power_rows[m].T, lower=True).T)
    col_terms = jnp.stack([jnp.dot(blocks[m].T, hats[m], precision=highest) for m in range(3)])
    q_new = lax.psum(col_terms, ("node", "grp")) / group_count
    errors = [blocks[m] - jnp.dot(hats[m], q_new[m].T, precision=highest) for m in range(3)]
    new_error = jnp.concatenate(errors, axis=1).astype(jnp.bfloat16)[None]
    return (token_grad, new_error, jnp.stack(hats), q_new)


def solution(mesh):
    return jax.shard_map(
        on_device,
        mesh=mesh,
        in_specs=(
            P(("node", "grp"), None),
            P(("node", "grp"), None),
            P("node", None),
            P("node", None),
            P("node", None),
            P("grp", "node", None),
            P(),
        ),
        out_specs=(P(("node", "grp"), None), P("grp", "node", None), P(None, "node", None), P()),
        check_vma=False,
    )
```

profile of v0, /device:TPU:0, one launch (start us, length us, event | category | flops | bytes accessed | tf_op | source)
XLA Modules:
  0.0 512.1 jit_solution(15546751805123783097)
XLA Ops:
  9.4 37.6 %all-gather.6.cloned.1.call-done = bf16[1792,1024]{1,0:T(8,128)(2,1)} async-done(((bf16[224,1024]{1,0:T(8,128)(2,1)}), bf16[1792,1024]{1,0:T(8,128)(2,1)}) %all-gather.6.cloned.1.call-update) | async-done | bytes 3670032 | tf_op jit(solution)/shard_map/all_gather | solution.py:33
  47.0 5.2 %fusion.44 = f32[384,1024]{1,0:T(8,128)} fusion(bf16[384,1792]{1,0:T(8,128)(2,1)} %param.11, bf16[1792,1024]{1,0:T(8,128)(2,1)} %all-gather.6.cloned.1.call-done), kind=kOutput, calls=%fused_computation.92 | convolution fusion | flops 1409286144 | bytes 6619136 | tf_op jit(solution)/shard_map/dot_general | solution.py:39
  52.2 31.1 %all-gather.10.cloned.1.call-done = bf16[1792,1024]{1,0:T(8,128)(2,1)} async-done(((bf16[224,1024]{1,0:T(8,128)(2,1)}), bf16[1792,1024]{1,0:T(8,128)(2,1)}) %all-gather.10.cloned.1.call-update) | async-done | bytes 3670032 | tf_op jit(solution)/shard_map/all_gather | solution.py:31
  83.3 4.8 fusion.45
  88.1 31.5 %all-gather.8.cloned.1.call-done = bf16[1792,1024]{1,0:T(8,128)(2,1)} async-done(((bf16[224,1024]{1,0:T(8,128)(2,1)}), bf16[1792,1024]{1,0:T(8,128)(2,1)}) %all-gather.8.cloned.1.call-update) | async-done | bytes 3670032 | tf_op jit(solution)/shard_map/all_gather | solution.py:32
  119.6 6.4 %multiply_convert_fusion = (bf16[384,1024]{1,0:T(8,128)(2,1)}, bf16[384,1024]{1,0:T(8,128)(2,1)S(1)}, bf16[384,1024]{1,0:T(8,128)(2,1)S(1)}) fusion(f32[384,1024]{1,0:T(8,128)} %fusion.45, f32[384,1024]{1,0:T(8,128)} %fusion.44, bf16[384,1792]{1,0:T(8,128)(2,1)S(1)} %copy-done.2, bf16[1792,1024]{1,0:T(8,128)(2,1)} %all-gather.8.cloned.1.call-done), kind=kOutput, calls=%fused_computation.15 | convolution fusion | flops 1419116544 | bytes 10551296 | tf_op jit(solution)/shard_map/dot_general | solution.py:36
  129.6 1.5 copy.17
  131.1 3.6 all-to-all-start.1
  134.7 1.5 copy.15
  136.3 24.3 %all-to-all-done.1 = bf16[384,8,224]{0,2,1:T(8,128)(2,1)S(1)} async-done(((bf16[384,8,224]{0,2,1:T(8,128)(2,1)}), bf16[384,8,224]{0,2,1:T(8,128)(2,1)S(1)}, u32[]{:S(2)}, u32[]{:S(2)}) %all-to-all-start.1) | async-done | bytes 1376288 | tf_op jit(solution)/shard_map/all_to_all | solution.py:53
  160.5 3.6 all-to-all-start
  165.7 31.9 %all-to-all-done = bf16[384,8,224]{0,2,1:T(8,128)(2,1)S(1)} async-done(((bf16[384,8,224]{0,2,1:T(8,128)(2,1)}), bf16[384,8,224]{0,2,1:T(8,128)(2,1)S(1)}, u32[]{:S(2)}, u32[]{:S(2)}) %all-to-all-start) | async-done | bytes 1376288 | tf_op jit(solution)/shard_map/all_to_all | solution.py:52
  198.9 5.4 %fusion.46 = f32[384,1792]{1,0:T(8,128)} fusion(bf16[384,1024]{1,0:T(8,128)(2,1)S(1)} %copy-done.8, bf16[1792,1024]{1,0:T(8,128)(2,1)} %all-gather.10.cloned.1.call-done), kind=kOutput, calls=%fused_computation.94 | convolution fusion | flops 1409286144 | bytes 7208960 | tf_op jit(solution)/shard_map/dot_general | solution.py:43
  204.3 5.4 %convolution_bitcast_fusion.1 = f32[224,1024]{1,0:T(8,128)} fusion(bf16[3072,224]{0,1:T(8,128)(2,1)S(1)} %bitcast.133, bf16[3072,1024]{1,0:T(8,128)(2,1)} %all-gather.14.cloned.1.call-done), kind=kOutput, calls=%fused_computation.19 | convolution fusion | flops 1409286144 | bytes 8585216 | tf_op jit(solution)/shard_map/dot_general | solution.py:20
  209.7 64.7 %all-gather.12.cloned.1.call-done = bf16[3072,2048]{1,0:T(8,128)(2,1)} async-done(((bf16[384,2048]{1,0:T(8,128)(2,1)}), bf16[3072,2048]{1,0:T(8,128)(2,1)}) %all-gather.12.cloned.1.call-update) | async-done | bytes 12582928 | tf_op jit(solution)/shard_map/all_gather | solution.py:55
  274.4 6.4 %convolution_bitcast_fusion = f32[224,2048]{1,0:T(8,128)S(1)} fusion(bf16[3072,224]{0,1:T(8,128)(2,1)S(1)} %bitcast.134, bf16[3072,2048]{1,0:T(8,128)(2,1)} %all-gather.12.cloned.1.call-done), kind=kOutput, calls=%fused_computation.4 | convolution fusion | flops 2818572288 | bytes 15794176 | tf_op jit(solution)/shard_map/dot_general | solution.py:20
  285.2 20.5 %psum.21 = bf16[3,224,32]{1,2,0:T(8,128)(2,1)} all-reduce(bf16[3,224,32]{1,2,0:T(8,128)(2,1)} %pad_maximum_fusion.4), channel_id=1, replica_groups=mesh['node'=8,'grp'=4] {'grp'}, use_global_device_ids=true, to_apply=%region_0.0 | all-reduce | flops 21504 | bytes 86016 | tf_op jit(solution)/shard_map/psum | solution.py:64
  305.6 1.7 fusion.33
  307.4 1.4 convert_multiply_fusion
  308.8 24.0 %psum.22 = f32[3,32,32]{1,2,0:T(8,128)} all-reduce(f32[3,32,32]{1,2,0:T(8,128)} %fusion.33), channel_id=1, replica_groups=mesh['node'=8,'grp'=4] {'node'}, use_global_device_ids=true, to_apply=%region_1.0 | all-reduce | flops 3072 | bytes 24576 | tf_op jit(solution)/shard_map/psum | solution.py:66
  339.2 3.6 cholesky.59
  344.8 3.8 custom-call.7
  348.5 3.6 cholesky.70
  354.1 3.2 custom-call.8
  357.3 1.6 fusion.32
  358.9 1.6 fusion.31
  360.5 3.6 cholesky.81
  366.0 3.2 custom-call.9
  370.9 1.4 convolution_bitcast_fusion.3
  373.8 5.7 %fusion = bf16[384,1792]{1,0:T(8,128)(2,1)} fusion(f32[384,1792]{1,0:T(8,128)} %fusion.46, bf16[384,1024]{1,0:T(8,128)(2,1)S(1)} %get-tuple-element.8, bf16[1792,1024]{1,0:T(8,128)(2,1)} %all-gather.8.cloned.1.call-done), kind=kOutput, calls=%fused_computation.1 | convolution fusion | flops 1410662400 | bytes 8585216 | tf_op jit(solution)/shard_map/dot_general | solution.py:46
  380.2 119.2 %all-reduce.2.cloned.1.call-done = f32[3,1024,32]{1,2,0:T(8,128)} async-done(((f32[3,1024,32]{1,2,0:T(8,128)}), f32[3,1024,32]{1,2,0:T(8,128)}) %all-reduce.2.cloned.1.call-update) | async-done | bytes 393232 | tf_op jit(solution)/shard_map/psum | solution.py:72
  500.4 1.8 fusion.12
  (78 shorter events, 33.0 us)
Async XLA Ops:
  7.2 39.8 %all-gather.6.cloned.1.call-start = ((), (), s32[]{:S(2)}) async-start(), calls=%async_computation.2 | async-start | bytes 4128768 | tf_op jit(solution)/shard_map/all_gather | solution.py:33
  7.9 75.4 %all-gather.10.cloned.1.call-start = ((), (), s32[]{:S(2)}) async-start(), calls=%async_computation.4 | async-start | bytes 4128768 | tf_op jit(solution)/shard_map/all_gather | solution.py:31
  8.6 111.0 %all-gather.8.cloned.1.call-start = ((), (), s32[]{:S(2)}) async-start(), calls=%async_computation.3 | async-start | bytes 4128768 | tf_op jit(solution)/shard_map/all_gather | solution.py:32
  9.4 73.9 %copy-start.2 = (bf16[384,1792]{1,0:T(8,128)(2,1)S(1)}, bf16[384,1792]{1,0:T(8,128)(2,1)}, u32[]{:S(2)}) copy-start(bf16[384,1792]{1,0:T(8,128)(2,1)} %param.10) | copy-start | bytes 4128772
  9.4 194.9 %all-gather.14.cloned.1.call-start = ((), (), s32[]{:S(2)}) async-start(), calls=%async_computation.6 | async-start | bytes 7077888 | tf_op jit(solution)/shard_map/all_gather | solution.py:56
  126.0 0.9 copy-start.7
  126.0 148.4 %all-gather.12.cloned.1.call-start = ((), (), s32[]{:S(2)}) async-start(), calls=%async_computation.5 | async-start | bytes 14155776 | tf_op jit(solution)/shard_map/all_gather | solution.py:55
  128.2 1.3 copy-start.1
  131.1 29.4 %all-to-all-start.1 = ((bf16[384,8,224]{0,2,1:T(8,128)(2,1)}), bf16[384,8,224]{0,2,1:T(8,128)(2,1)S(1)}, u32[]{:S(2)}, u32[]{:S(2)}) async-start(bf16[384,8,224]{0,2,1:T(8,128)(2,1)} %bitcast.3), calls=%async_computation.1 | async-start | bytes 2752512 | tf_op jit(solution)/shard_map/all_to_all | solution.py:53
  160.5 37.1 %all-to-all-start = ((bf16[384,8,224]{0,2,1:T(8,128)(2,1)}), bf16[384,8,224]{0,2,1:T(8,128)(2,1)S(1)}, u32[]{:S(2)}, u32[]{:S(2)}) async-start(bf16[384,8,224]{0,2,1:T(8,128)(2,1)} %bitcast), calls=%async_computation | async-start | bytes 2752512 | tf_op jit(solution)/shard_map/all_to_all | solution.py:52
  164.1 335.3 %all-reduce.2.cloned.1.call-start = ((), (), s32[]{:S(2)}) async-start(), calls=%async_computation.7 | async-start | bytes 786432 | tf_op jit(solution)/shard_map/psum | solution.py:72
  197.6 1.3 copy-start.8
  198.9 5.4 %copy-start.4 = (bf16[8,28,8,384]{3,2,0,1:T(8,128)(2,1)S(1)}, bf16[8,28,8,384]{3,2,0,1:T(8,128)(2,1)}, u32[]{:S(2)}) copy-start(bf16[8,28,8,384]{3,2,0,1:T(8,128)(2,1)} %copy.25) | copy-start | bytes 4128772
  204.3 70.1 %copy-start.5 = (bf16[8,28,8,384]{3,2,0,1:T(8,128)(2,1)S(1)}, bf16[8,28,8,384]{3,2,0,1:T(8,128)(2,1)}, u32[]{:S(2)}) copy-start(bf16[8,28,8,384]{3,2,0,1:T(8,128)(2,1)} %copy.24) | copy-start | bytes 4128772
  274.4 6.4 %copy-start.3 = (bf16[1,224,3072]{2,1,0:T(8,128)(2,1)S(1)}, bf16[1,224,3072]{2,1,0:T(8,128)(2,1)}, u32[]{:S(2)}) copy-start(bf16[1,224,3072]{2,1,0:T(8,128)(2,1)} %param.15) | copy-start | bytes 4128772
  274.4 6.4 %copy-start.6 = (f32[224,1024]{1,0:T(8,128)S(1)}, f32[224,1024]{1,0:T(8,128)}, u32[]{:S(2)}) copy-start(f32[224,1024]{1,0:T(8,128)} %convolution_bitcast_fusion.1) | copy-start | bytes 2752516
  280.8 1.0 copy-start.16
  369.2 3.1 copy-start.9
  370.2 2.8 copy-start.14
  373.8 5.7 %copy-start.10 = (f32[32,224]{1,0:T(8,128)S(1)}, f32[32,224]{1,0:T(8,128)}, u32[]{:S(2)}) copy-start(f32[32,224]{1,0:T(8,128)} %fusion.32) | copy-start | bytes 86020
  373.8 5.7 %copy-start.12 = (f32[32,224]{1,0:T(8,128)S(1)}, f32[32,224]{1,0:T(8,128)}, u32[]{:S(2)}) copy-start(f32[32,224]{1,0:T(8,128)} %fusion.31) | copy-start | bytes 86020
  373.8 5.7 %copy-start.15 = (f32[32,224]{1,0:T(8,128)S(1)}, f32[32,224]{1,0:T(8,128)}, u32[]{:S(2)}) copy-start(f32[32,224]{1,0:T(8,128)} %copy-done.14) | copy-start | bytes 86020
  379.5 122.7 %copy-start.13 = (f32[32,224]{1,0:T(8,128)S(1)}, f32[32,224]{1,0:T(8,128)}, u32[]{:S(2)}) copy-start(f32[32,224]{1,0:T(8,128)} %fusion.31) | copy-start | bytes 86020
  500.4 3.7 copy-start
  500.4 2.7 copy-start.11
Sparse Core Ops, SparseCore 0:
  9.9 37.0 all-gather.5
  48.9 34.3 all-gather.9
  85.2 34.3 all-gather.7
  126.1 74.4 all-gather.13
  202.4 71.9 all-gather.11
  373.9 125.4 all-reduce.1
where the time goes:
time: 514 us; the launch traced here: 512 us
  waiting for transfers between devices  342 us (67%)
  matrix products  54.2 us (11%)
  blocking collectives  44.5 us (9%)
  other arithmetic  35.7 us (7%)
  between operations  14.4 us (3%)
  local copies, waits for them, and re-layouts  13.4 us (3%)
  starting transfers between devices  7.6 us (1%)
    psum x1, waiting for transfers between devices, on_device(): q_new = lax.psum(col_terms, ('node', 'grp')) / group_count  119 us
    all_gather x1, waiting for transfers between devices, on_device(): piece_gu = lax.all_gather(gate_up, 'node', axis=0, tiled=True)  64.7 us
    all_gather x1, waiting for transfers between devices, on_device(): lax.all_gather(down_weight_t, 'node', axis=0, tiled=True)  37.6 us
    all_to_all x1, waiting for transfers between devices, on_device(): lax.all_to_all(tokens, 'node', split_axis=1, concat_axis=0, tiled=True)  31.9 us
    all_gather x1, waiting for transfers between devices, on_device(): lax.all_gather(up_weight, 'node', axis=0, tiled=True)  31.5 us
    all_gather x1, waiting for transfers between devices, on_device(): lax.all_gather(gate_weight, 'node', axis=0, tiled=True)  31.1 us
    all_to_all x1, waiting for transfers between devices, on_device(): lax.all_to_all(cotangent, 'node', split_axis=1, concat_axis=0, tiled=True)  24.3 us
    psum x1, blocking collectives, on_device(): gram_matrix = lax.psum(local_gram, 'node')  24 us
  transfers between devices with their start and end apart: 8, of which 7 were waited for; matrix products, arithmetic and copies ran while one was open for 7% of the time, Pallas kernels for 0%

commit v1 on v0

--- a/solution.py
+++ b/solution.py
@@ -52,8 +52,11 @@
         lax.all_to_all(tokens, "node", split_axis=1, concat_axis=0, tiled=True),
         lax.all_to_all(cotangent, "node", split_axis=1, concat_axis=0, tiled=True),
     )
-    piece_gu = lax.all_gather(gate_up, "node", axis=0, tiled=True)
-    piece_hidden = lax.all_gather(hidden, "node", axis=0, tiled=True)
+    piece_gu, piece_hidden = jnp.split(
+        lax.all_gather(jnp.concatenate([gate_up, hidden], axis=1), "node", axis=0, tiled=True),
+        [gate_up.shape[1]],
+        axis=1,
+    )
     summed = jnp.concatenate(
         [contract_rows(token_cols, piece_gu), contract_rows(cot_cols, piece_hidden)], axis=1
     )

time: 514 us -> 495 us (0.963)
  waiting for transfers between devices: 342 us -> 325 us
    all_gather x2 -> x1, waiting for transfers between devices: 64.7 us -> 51.8 us  [on_device(): lax.all_gather(jnp.concatenate([gate_up, hidden], axis=1), 'node', axis=0...]
    all_to_all x1, waiting for transfers between devices: 31.9 us -> 23.5 us  [on_device(): lax.all_to_all(tokens, 'node', split_axis=1, concat_axis=0, tiled=True)]
    all_gather x1, waiting for transfers between devices: 31.1 us -> 37.6 us  [on_device(): lax.all_gather(gate_weight, 'node', axis=0, tiled=True)]
    all_gather x1, waiting for transfers between devices: 37.6 us -> 31.1 us  [on_device(): lax.all_gather(down_weight_t, 'node', axis=0, tiled=True)]
  transfers between devices with their start and end apart: 8 -> 7, of which waited for: 7 -> 7; matrix products, arithmetic and copies ran while one was open for 7% -> 6% of each run, Pallas kernels for 0% -> 0%
where the time goes in v1:
time: 495 us; the launch traced here: 494 us
  waiting for transfers between devices  325 us (66%)
  matrix products  51.8 us (10%)
  blocking collectives  44.5 us (9%)
  other arithmetic  36.6 us (7%)
  between operations  14.1 us (3%)
  local copies, waits for them, and re-layouts  14 us (3%)
  starting transfers between devices  7.52 us (2%)
    psum x1, waiting for transfers between devices, on_device(): q_new = lax.psum(col_terms, ('node', 'grp')) / group_count  119 us
    all_gather x1, waiting for transfers between devices, on_device(): lax.all_gather(jnp.concatenate([gate_up, hidden], axis=1), 'node', axis=0...  51.8 us
    all_gather x1, waiting for transfers between devices, on_device(): lax.all_gather(gate_weight, 'node', axis=0, tiled=True)  37.6 us
    all_gather x1, waiting for transfers between devices, on_device(): lax.all_gather(up_weight, 'node', axis=0, tiled=True)  31.5 us
    all_gather x1, waiting for transfers between devices, on_device(): lax.all_gather(down_weight_t, 'node', axis=0, tiled=True)  31.1 us
    all_to_all x1, waiting for transfers between devices, on_device(): lax.all_to_all(cotangent, 'node', split_axis=1, concat_axis=0, tiled=True)  28.6 us
    psum x1, blocking collectives, on_device(): gram_matrix = lax.psum(local_gram, 'node')  24 us
    all_to_all x1, waiting for transfers between devices, on_device(): lax.all_to_all(tokens, 'node', split_axis=1, concat_axis=0, tiled=True)  23.5 us
  transfers between devices with their start and end apart: 7, of which 7 were waited for; matrix products, arithmetic and copies ran while one was open for 6% of the time, Pallas kernels for 0%

profile of v1, /device:TPU:0, one launch (start us, length us, event | category | flops | bytes accessed | tf_op | source)
XLA Modules:
  0.0 493.6 jit_solution(3378412146468908143)
XLA Ops:
  9.4 37.6 %all-gather.9.cloned.1.call-done = bf16[1792,1024]{1,0:T(8,128)(2,1)} async-done(((bf16[224,1024]{1,0:T(8,128)(2,1)}), bf16[1792,1024]{1,0:T(8,128)(2,1)}) %all-gather.9.cloned.1.call-update) | async-done | bytes 3670032 | tf_op jit(solution)/shard_map/all_gather | solution.py:31
  47.0 5.2 %fusion.55 = f32[384,1024]{1,0:T(8,128)} fusion(bf16[384,1792]{1,0:T(8,128)(2,1)} %param.10, bf16[1792,1024]{1,0:T(8,128)(2,1)} %all-gather.9.cloned.1.call-done), kind=kOutput, calls=%fused_computation.97 | convolution fusion | flops 1409286144 | bytes 6619136 | tf_op jit(solution)/shard_map/dot_general | solution.py:35
  52.2 31.1 %all-gather.5.cloned.1.call-done = bf16[1792,1024]{1,0:T(8,128)(2,1)} async-done(((bf16[224,1024]{1,0:T(8,128)(2,1)}), bf16[1792,1024]{1,0:T(8,128)(2,1)}) %all-gather.5.cloned.1.call-update) | async-done | bytes 3670032 | tf_op jit(solution)/shard_map/all_gather | solution.py:33
  83.3 4.8 fusion.54
  88.1 31.5 %all-gather.7.cloned.1.call-done = bf16[1792,1024]{1,0:T(8,128)(2,1)} async-done(((bf16[224,1024]{1,0:T(8,128)(2,1)}), bf16[1792,1024]{1,0:T(8,128)(2,1)}) %all-gather.7.cloned.1.call-update) | async-done | bytes 3670032 | tf_op jit(solution)/shard_map/all_gather | solution.py:32
  119.6 5.5 %multiply_convert_fusion = (bf16[384,1024]{1,0:T(8,128)(2,1)S(1)}, bf16[384,1024]{1,0:T(8,128)(2,1)S(1)}, bf16[384,1024]{1,0:T(8,128)(2,1)S(1)}) fusion(f32[384,1024]{1,0:T(8,128)} %fusion.55, f32[384,1024]{1,0:T(8,128)} %fusion.54, bf16[384,1792]{1,0:T(8,128)(2,1)S(1)} %copy-done.2, bf16[1792,1024]{1,0:T(8,128)(2,1)} %all-gather.7.cloned.1.call-done), kind=kOutput, calls=%fused_computation.19 | convolution fusion | flops 1419116544 | bytes 10551296 | tf_op jit(solution)/shard_map/dot_general | solution.py:36
  126.0 1.6 pad_maximum_fusion
  127.6 1.5 copy.17
  129.1 3.6 all-to-all-start.1
  132.7 1.5 copy.15
  134.3 28.6 %all-to-all-done.1 = bf16[384,8,224]{0,2,1:T(8,128)(2,1)S(1)} async-done(((bf16[384,8,224]{0,2,1:T(8,128)(2,1)}), bf16[384,8,224]{0,2,1:T(8,128)(2,1)S(1)}, u32[]{:S(2)}, u32[]{:S(2)}) %all-to-all-start.1) | async-done | bytes 1376288 | tf_op jit(solution)/shard_map/all_to_all | solution.py:53
  162.8 3.6 all-to-all-start
  168.0 23.5 %all-to-all-done = bf16[384,8,224]{0,2,1:T(8,128)(2,1)S(1)} async-done(((bf16[384,8,224]{0,2,1:T(8,128)(2,1)}), bf16[384,8,224]{0,2,1:T(8,128)(2,1)S(1)}, u32[]{:S(2)}, u32[]{:S(2)}) %all-to-all-start) | async-done | bytes 1376288 | tf_op jit(solution)/shard_map/all_to_all | solution.py:52
  192.8 5.5 %fusion.56 = f32[384,1792]{1,0:T(8,128)} fusion(bf16[384,1024]{1,0:T(8,128)(2,1)S(1)} %copy-done.7, bf16[1792,1024]{1,0:T(8,128)(2,1)} %all-gather.9.cloned.1.call-done), kind=kOutput, calls=%fused_computation.98 | convolution fusion | flops 1409286144 | bytes 7208960 | tf_op jit(solution)/shard_map/dot_general | solution.py:43
  198.4 51.8 %all-gather.11.cloned.1.call-done = bf16[3072,3072]{1,0:T(8,128)(2,1)} async-done(((bf16[384,3072]{1,0:T(8,128)(2,1)}), bf16[3072,3072]{1,0:T(8,128)(2,1)}) %all-gather.11.cloned.1.call-update) | async-done | bytes 18874384 | tf_op jit(solution)/shard_map/all_gather | solution.py:56
  250.2 4.5 fusion.16
  254.7 6.3 %fusion.6 = f32[224,2048]{1,0:T(8,128)S(1)} fusion(bf16[3072,224]{0,1:T(8,128)(2,1)S(1)} %bitcast.132, bf16[3072,3072]{1,0:T(8,128)(2,1)} %all-gather.11.cloned.1.call-done), kind=kOutput, calls=%fused_computation.8 | convolution fusion | flops 2818572288 | bytes 15794176 | tf_op jit(solution)/shard_map/dot_general | solution.py:20
  265.4 20.5 %psum.21 = bf16[3,224,32]{1,2,0:T(8,128)(2,1)} all-reduce(bf16[3,224,32]{1,2,0:T(8,128)(2,1)} %pad_maximum_fusion.4), channel_id=1, replica_groups=mesh['node'=8,'grp'=4] {'grp'}, use_global_device_ids=true, to_apply=%region_0.0 | all-reduce | flops 21504 | bytes 86016 | tf_op jit(solution)/shard_map/psum | solution.py:67
  285.8 1.4 convert_multiply_fusion
  287.3 1.7 fusion.43
  289.0 24.0 %psum.22 = f32[3,32,32]{1,2,0:T(8,128)} all-reduce(f32[3,32,32]{1,2,0:T(8,128)} %fusion.43), channel_id=1, replica_groups=mesh['node'=8,'grp'=4] {'node'}, use_global_device_ids=true, to_apply=%region_1.0 | all-reduce | flops 3072 | bytes 24576 | tf_op jit(solution)/shard_map/psum | solution.py:69
  318.0 1.4 fusion.49
  319.4 3.6 cholesky.81
  325.1 3.2 custom-call.9
  331.2 3.6 cholesky.70
  336.9 3.2 custom-call.8
  343.0 3.6 cholesky.59
  348.7 3.2 custom-call.7
  354.1 1.7 pad_maximum_fusion.2
  355.9 5.7 %fusion.4 = bf16[384,1792]{1,0:T(8,128)(2,1)} fusion(f32[384,1792]{1,0:T(8,128)} %fusion.56, bf16[384,1024]{1,0:T(8,128)(2,1)S(1)} %get-tuple-element.8, bf16[1792,1024]{1,0:T(8,128)(2,1)} %all-gather.7.cloned.1.call-done), kind=kOutput, calls=%fused_computation.5 | convolution fusion | flops 1410662400 | bytes 8585216 | tf_op jit(solution)/shard_map/dot_general | solution.py:46
  362.3 119.0 %all-reduce.2.cloned.1.call-done = f32[3,1024,32]{1,2,0:T(8,128)} async-done(((f32[3,1024,32]{1,2,0:T(8,128)}), f32[3,1024,32]{1,2,0:T(8,128)}) %all-reduce.2.cloned.1.call-update) | async-done | bytes 393232 | tf_op jit(solution)/shard_map/psum | solution.py:75
  482.3 1.7 fusion.22
  (75 shorter events, 34.2 us)
Async XLA Ops:
  7.2 39.8 %all-gather.9.cloned.1.call-start = ((), (), s32[]{:S(2)}) async-start(), calls=%async_computation.4 | async-start | bytes 4128768 | tf_op jit(solution)/shard_map/all_gather | solution.py:31
  7.9 75.4 %all-gather.5.cloned.1.call-start = ((), (), s32[]{:S(2)}) async-start(), calls=%async_computation.2 | async-start | bytes 4128768 | tf_op jit(solution)/shard_map/all_gather | solution.py:33
  8.6 111.0 %all-gather.7.cloned.1.call-start = ((), (), s32[]{:S(2)}) async-start(), calls=%async_computation.3 | async-start | bytes 4128768 | tf_op jit(solution)/shard_map/all_gather | solution.py:32
  9.4 73.9 %copy-start.1 = (bf16[384,1792]{1,0:T(8,128)(2,1)S(1)}, bf16[384,1792]{1,0:T(8,128)(2,1)}, u32[]{:S(2)}) copy-start(bf16[384,1792]{1,0:T(8,128)(2,1)} %param.11) | copy-start | bytes 4128772
  9.4 240.8 %all-gather.11.cloned.1.call-start = ((), (), s32[]{:S(2)}) async-start(), calls=%async_computation.5 | async-start | bytes 21233664 | tf_op jit(solution)/shard_map/all_gather | solution.py:56
  52.2 67.4 %copy-start.2 = (bf16[384,1792]{1,0:T(8,128)(2,1)S(1)}, bf16[384,1792]{1,0:T(8,128)(2,1)}, u32[]{:S(2)}) copy-start(bf16[384,1792]{1,0:T(8,128)(2,1)} %param.10) | copy-start | bytes 4128772
  125.1 0.9 copy-start.6
  129.1 33.7 %all-to-all-start.1 = ((bf16[384,8,224]{0,2,1:T(8,128)(2,1)}), bf16[384,8,224]{0,2,1:T(8,128)(2,1)S(1)}, u32[]{:S(2)}, u32[]{:S(2)}) async-start(bf16[384,8,224]{0,2,1:T(8,128)(2,1)} %bitcast.3), calls=%async_computation.1 | async-start | bytes 2752512 | tf_op jit(solution)/shard_map/all_to_all | solution.py:53
  162.8 28.7 %all-to-all-start = ((bf16[384,8,224]{0,2,1:T(8,128)(2,1)}), bf16[384,8,224]{0,2,1:T(8,128)(2,1)S(1)}, u32[]{:S(2)}, u32[]{:S(2)}) async-start(bf16[384,8,224]{0,2,1:T(8,128)(2,1)} %bitcast), calls=%async_computation | async-start | bytes 2752512 | tf_op jit(solution)/shard_map/all_to_all | solution.py:52
  166.4 314.8 %all-reduce.2.cloned.1.call-start = ((), (), s32[]{:S(2)}) async-start(), calls=%async_computation.6 | async-start | bytes 786432 | tf_op jit(solution)/shard_map/psum | solution.py:75
  168.0 24.9 %copy-start.7 = (bf16[384,1024]{1,0:T(8,128)(2,1)S(1)}, bf16[384,1024]{1,0:T(8,128)(2,1)}, u32[]{:S(2)}) copy-start(bf16[384,1024]{1,0:T(8,128)(2,1)} %copy-done.6) | copy-start | bytes 2359300
  192.8 57.3 %copy-start.4 = (bf16[8,28,8,384]{3,2,0,1:T(8,128)(2,1)S(1)}, bf16[8,28,8,384]{3,2,0,1:T(8,128)(2,1)}, u32[]{:S(2)}) copy-start(bf16[8,28,8,384]{3,2,0,1:T(8,128)(2,1)} %copy.25) | copy-start | bytes 4128772
  250.2 4.5 copy-start.5
  254.7 6.4 %copy-start.3 = (bf16[1,224,3072]{2,1,0:T(8,128)(2,1)S(1)}, bf16[1,224,3072]{2,1,0:T(8,128)(2,1)}, u32[]{:S(2)}) copy-start(bf16[1,224,3072]{2,1,0:T(8,128)(2,1)} %param.15) | copy-start | bytes 4128772
  261.0 1.0 copy-start.16
  329.3 0.6 copy-start.8
  341.0 0.6 copy-start.10
  352.8 0.6 copy-start.13
  355.9 5.7 %copy-start.9 = (f32[32,224]{1,0:T(8,128)S(1)}, f32[32,224]{1,0:T(8,128)}, u32[]{:S(2)}) copy-start(f32[32,224]{1,0:T(8,128)} %copy-done.8) | copy-start | bytes 86020
  355.9 5.7 %copy-start.11 = (f32[32,224]{1,0:T(8,128)S(1)}, f32[32,224]{1,0:T(8,128)}, u32[]{:S(2)}) copy-start(f32[32,224]{1,0:T(8,128)} %copy-done.10) | copy-start | bytes 86020
  355.9 5.7 %copy-start.14 = (f32[32,224]{1,0:T(8,128)S(1)}, f32[32,224]{1,0:T(8,128)}, u32[]{:S(2)}) copy-start(f32[32,224]{1,0:T(8,128)} %copy-done.13) | copy-start | bytes 86020
  361.6 122.4 %copy-start.12 = (f32[32,224]{1,0:T(8,128)S(1)}, f32[32,224]{1,0:T(8,128)}, u32[]{:S(2)}) copy-start(f32[32,224]{1,0:T(8,128)} %copy-done.10) | copy-start | bytes 86020
  361.6 123.3 %copy-start.15 = (f32[32,224]{1,0:T(8,128)S(1)}, f32[32,224]{1,0:T(8,128)}, u32[]{:S(2)}) copy-start(f32[32,224]{1,0:T(8,128)} %copy-done.13) | copy-start | bytes 86020
  482.2 4.8 copy-start
Sparse Core Ops, SparseCore 0:
  9.9 37.0 all-gather.8
  48.9 34.3 all-gather.4
  85.2 34.3 all-gather.6
  127.7 122.3 all-gather.10
  356.0 125.1 all-reduce.1
